TPU v7x, 32 devices: a whole 2x2x4 slice. The times are simulated.
32 devices in a mesh: dev: 32 (over z, y, x, core).
Axes of the slice: x: 2, y: 2, z: 4, core: 2. Of those that a mesh axis runs over, the one named last changes fastest.
Arguments:
- gauss_params: float32 [59, 262144], P(None, 'dev'), may hold values from -8 to 8, as said below
- adam_first: float32 [59, 262144], P(None, 'dev'), may hold values from -6 to 6
- adam_second: float32 [59, 262144], P(None, 'dev'), may hold values from 0.0001 to 100
- camera: float32 [2, 6], replicated, may hold values from -0.004 to 0.004
- send_first: int32 [32, 4096], P('dev'), may hold values from -1 to 8191, as said below
- send_second: int32 [32, 4096], P('dev'), may hold values from -1 to 8191, as said below
- lists_first: int32 [1024, 128], P('dev'), may hold values from -1 to 4095, as said below
- lists_second: int32 [1024, 128], P('dev'), may hold values from -1 to 4095, as said below
- tiles_first: int32 [1024], P('dev'), may hold values from 0 to 1023, as said below
- tiles_second: int32 [1024], P('dev'), may hold values from 0 to 1023, as said below
- targets: float32 [1024, 3, 256], P('dev'), may hold values from 0 to 1
Outputs:
- new_params: float32 [59, 262144], P(None, 'dev')
- new_first: float32 [59, 262144], P(None, 'dev')
- new_second: float32 [59, 262144], P(None, 'dev')
- rendered_next: float32 [1024, 3, 256], P('dev')
Inputs may be any that keep to these rules, and one draw needn't show every extreme that they name: `gauss_params`: rows 0 to 2 hold a position, 3 to 5 log scales, 6 to 9 a quaternion (w, x, y, z) with w at least 1, 10 an opacity logit, 11 + 16 c + k the spherical-harmonic coefficient k of colour c. Every Gaussian lies at depth 1.4 or more in front of both cameras. `send_first`: row s holds, for each destination d in turn, 128 slots: local column indices of Gaussians of device s, the used ones first, then -1. Entries other than -1 in a row are distinct. Some destination gets 128 used slots from every device. `send_second`: same form as send_first, but unused slots (-1) may stand anywhere in a destination's run. Some destination gets 128 used slots from every device. `lists_first`: row r, rendered by device r // 32, lists in compositing order (front first) received slots s * 128 + k of that device (slot k from device s), only used slots, then -1 to the end. Every used slot of a device appears exactly once among its rows. Some rows have no -1. `lists_second`: same form as lists_first, for the next view and its send array. `tiles_first`: A permutation of the image's tiles. `tiles_second`: A permutation of the image's tiles.
All inputs are finite; a program needn't handle non-finite values.
Results may differ from a plain program's by a relative error of at most 0.0003.
Values sent between devices are 32-bit elements; how exact they have to be, the bound alone decides.
No kernel may reach another device: no remote copies, remote signals or barrier semaphores. Data moves between devices by JAX's collectives and lax.ppermute only.
A program may use at most 128 MiB of HBM per device.

v0:
```python
import jax
import jax.numpy as jnp
import numpy as np
from jax import lax
from jax.sharding import PartitionSpec as P

LIST_LEN = 128
TILE_PIXELS = 256
TILES_X = 128
tile_edge = 16
focal_length = 1000.0
blur_floor = 0.3
adam_epsilon = 1e-08
bias_first = 1.0 - 0.9**20
bias_second = 1.0 - 0.999**20
sh_first = 0.28209479177387814
sh_second = 0.4886025119029199
sh_third = (
    1.0925484305920792,
    -1.0925484305920792,
    0.31539156525252005,
    -1.0925484305920792,
    0.5462742152960396,
)
sh_fourth = (
    -0.5900435899266435,
    2.890611442640554,
    -0.4570457994644658,
    0.3731763325901154,
    -0.4570457994644658,
    1.445305721320277,
    -0.5900435899266435,
)


def rate_values():
    values = np.full((59,), 0.000125)
    values[0:3] = 0.00016
    values[3:6] = 0.005
    values[6:10] = 0.001
    values[10] = 0.05
    values[11] = 0.0025
    values[27] = 0.0025
    values[43] = 0.0025
    return values


def camera_frame(camera_row):
    cosine_a, sine_a = (jnp.cos(camera_row[0]), jnp.sin(camera_row[0]))
    cosine_b, sine_b = (jnp.cos(camera_row[1]), jnp.sin(camera_row[1]))
    cosine_c, sine_c = (jnp.cos(camera_row[2]), jnp.sin(camera_row[2]))
    filler_zero = jnp.zeros_like(cosine_a)
    filler_one = jnp.ones_like(cosine_a)
    turn_x = jnp.stack(
        [
            jnp.stack([filler_one, filler_zero, filler_zero]),
            jnp.stack([filler_zero, cosine_a, -sine_a]),
            jnp.stack([filler_zero, sine_a, cosine_a]),
        ]
    )
    turn_y = jnp.stack(
        [
            jnp.stack([cosine_b, filler_zero, sine_b]),
            jnp.stack([filler_zero, filler_one, filler_zero]),
            jnp.stack([-sine_b, filler_zero, cosine_b]),
        ]
    )
    turn_z = jnp.stack(
        [
            jnp.stack([cosine_c, -sine_c, filler_zero]),
            jnp.stack([sine_c, cosine_c, filler_zero]),
            jnp.stack([filler_zero, filler_zero, filler_one]),
        ]
    )
    highest = lax.Precision.HIGHEST
    rotation = jnp.dot(turn_z, jnp.dot(turn_y, turn_x, precision=highest), precision=highest)
    return (rotation, camera_row[3:6])


def sh_terms(along_x, along_y, along_z):
    square_x, square_y, square_z = (along_x * along_x, along_y * along_y, along_z * along_z)
    return [
        -sh_second * along_y,
        sh_second * along_z,
        -sh_second * along_x,
        sh_third[0] * along_x * along_y,
        sh_third[1] * along_y * along_z,
        sh_third[2] * (2.0 * square_z - square_x - square_y),
        sh_third[3] * along_x * along_z,
        sh_third[4] * (square_x - square_y),
        sh_fourth[0] * along_y * (3.0 * square_x - square_y),
        sh_fourth[1] * along_x * along_y * along_z,
        sh_fourth[2] * along_y * (4.0 * square_z - square_x - square_y),
        sh_fourth[3] * along_z * (2.0 * square_z - 3.0 * square_x - 3.0 * square_y),
        sh_fourth[4] * along_x * (4.0 * square_z - square_x - square_y),
        sh_fourth[5] * along_z * (square_x - square_y),
        sh_fourth[6] * along_x * (square_x - 3.0 * square_y),
    ]


def project(params, camera_row, image_width, image_height):
    rotation, offset = camera_frame(camera_row)
    centres = params[0:3]
    viewed = [
        rotation[row_index, 0] * centres[0]
        + rotation[row_index, 1] * centres[1]
        + rotation[row_index, 2] * centres[2]
        + offset[row_index]
        for row_index in range(3)
    ]
    inverse_depth = 1.0 / viewed[2]
    screen_u = focal_length * viewed[0] * inverse_depth + 0.5 * image_width
    screen_v = focal_length * viewed[1] * inverse_depth + 0.5 * image_height
    scales = jnp.exp(params[3:6])
    versor = params[6:10] / jnp.sqrt(jnp.sum(params[6:10] * params[6:10], axis=0))
    part_w, part_x, part_y, part_z = (versor[0], versor[1], versor[2], versor[3])
    turn_rows = [
        [
            1.0 - 2.0 * (part_y * part_y + part_z * part_z),
            2.0 * (part_x * part_y - part_w * part_z),
            2.0 * (part_x * part_z + part_w * part_y),
        ],
        [
            2.0 * (part_x * part_y + part_w * part_z),
            1.0 - 2.0 * (part_x * part_x + part_z * part_z),
            2.0 * (part_y * part_z - part_w * part_x),
        ],
        [
            2.0 * (part_x * part_z - part_w * part_y),
            2.0 * (part_y * part_z + part_w * part_x),
            1.0 - 2.0 * (part_x * part_x + part_y * part_y),
        ],
    ]
    factor = [
        [turn_rows[row_index][col_index] * scales[col_index] for col_index in range(3)]
        for row_index in range(3)
    ]
    spread = [
        [
            factor[row_index][0] * factor[col_index][0]
            + factor[row_index][1] * factor[col_index][1]
            + factor[row_index][2] * factor[col_index][2]
            for col_index in range(3)
        ]
        for row_index in range(3)
    ]
    jacobian = [
        [
            focal_length * inverse_depth,
            0.0,
            -focal_length * viewed[0] * inverse_depth * inverse_depth,
        ],
        [
            0.0,
            focal_length * inverse_depth,
            -focal_length * viewed[1] * inverse_depth * inverse_depth,
        ],
    ]
    mapping = [
        [
            jacobian[row_index][0] * rotation[0, col_index]
            + jacobian[row_index][1] * rotation[1, col_index]
            + jacobian[row_index][2] * rotation[2, col_index]
            for col_index in range(3)
        ]
        for row_index in range(2)
    ]

    def mapped(first_index, second_index):
        running = 0.0
        for inner_a in range(3):
            for inner_b in range(3):
                running = (
                    running
                    + mapping[first_index][inner_a]
                    * spread[inner_a][inner_b]
                    * mapping[second_index][inner_b]
                )
        return running

    cover_a = mapped(0, 0) + blur_floor
    cover_b = mapped(0, 1)
    cover_c = mapped(1, 1) + blur_floor
    determinant = cover_a * cover_c - cover_b * cover_b
    opacity = jax.nn.sigmoid(params[10])
    centre_cam = [
        -(
            rotation[0, col_index] * offset[0]
            + rotation[1, col_index] * offset[1]
            + rotation[2, col_index] * offset[2]
        )
        for col_index in range(3)
    ]
    towards = [centres[col_index] - centre_cam[col_index] for col_index in range(3)]
    length = jnp.sqrt(towards[0] * towards[0] + towards[1] * towards[1] + towards[2] * towards[2])
    harmonics = sh_terms(towards[0] / length, towards[1] / length, towards[2] / length)
    colours = []
    for channel in range(3):
        running = 0.5 + sh_first * params[11 + 16 * channel]
        for term_index in range(1, 16):
            running = running + harmonics[term_index - 1] * params[11 + 16 * channel + term_index]
        colours.append(jnp.maximum(running, 0.0))
    return jnp.stack(
        [
            screen_u,
            screen_v,
            cover_c / determinant,
            -cover_b / determinant,
            cover_a / determinant,
            opacity,
        ]
        + colours
    )


def composite(gathered, live_mask, tile_numbers, triangle):
    pixel_ids = jnp.arange(TILE_PIXELS, dtype=jnp.int32)
    pixel_col = (tile_numbers % TILES_X)[:, None] * tile_edge + pixel_ids[None, :] % tile_edge
    pixel_row = (tile_numbers // TILES_X)[:, None] * tile_edge + pixel_ids[None, :] // tile_edge
    offset_x = gathered[0][:, None, :] - (pixel_col.astype(gathered.dtype) + 0.5)[:, :, None]
    offset_y = gathered[1][:, None, :] - (pixel_row.astype(gathered.dtype) + 0.5)[:, :, None]
    exponent = (
        -0.5
        * (
            gathered[2][:, None, :] * offset_x * offset_x
            + gathered[4][:, None, :] * offset_y * offset_y
        )
        - gathered[3][:, None, :] * offset_x * offset_y
    )
    coverage = gathered[5][:, None, :] * jnp.exp(exponent) * live_mask[:, None, :]
    log_clear = jnp.log1p(-coverage)
    before = jnp.einsum("bpj,ji->bpi", log_clear, triangle, precision=lax.Precision.HIGHEST)
    weight = coverage * jnp.exp(before)
    return jnp.einsum("bpi,cbi->bcp", weight, gathered[6:9], precision=lax.Precision.HIGHEST)


def group_of():
    return 8


def selector(width, ids, dtype):
    return (jnp.arange(width, dtype=jnp.int32)[:, None] == ids[None, :]).astype(dtype)


def block_inputs(buffer, tile_lists):
    live_mask = (tile_lists >= 0).astype(buffer.dtype)
    safe_ids = jnp.maximum(tile_lists, 0).reshape(-1)
    choose = selector(buffer.shape[1], safe_ids, buffer.dtype)
    gathered = jnp.dot(buffer, choose, precision=lax.Precision.HIGHEST).reshape(
        buffer.shape[0], tile_lists.shape[0], LIST_LEN
    )
    return (gathered, live_mask, choose)


def train_tiles(buffer, tile_lists, tile_numbers, targets, triangle):
    tile_group = group_of()
    block_count = tile_lists.shape[0] // tile_group

    def train_one_block(running, pieces):
        piece_lists, piece_tiles, piece_targets = pieces
        gathered, live_mask, choose = block_inputs(buffer, piece_lists)

        def block_loss(splat_block):
            rendered = composite(splat_block, live_mask, piece_tiles, triangle)
            return 0.5 * jnp.sum((rendered - piece_targets) ** 2)

        splat_grad = jax.grad(block_loss)(gathered) * live_mask[None, :, :]
        splat_grad = splat_grad.reshape(buffer.shape[0], tile_group * LIST_LEN)
        return (
            running
            + lax.dot_general(
                splat_grad, choose, (((1,), (1,)), ((), ())), precision=lax.Precision.HIGHEST
            ),
            None,
        )

    pieces = (
        tile_lists.reshape(block_count, tile_group, LIST_LEN),
        tile_numbers.reshape(block_count, tile_group),
        targets.reshape(block_count, tile_group, 3, TILE_PIXELS),
    )
    running, unused = lax.scan(train_one_block, jnp.zeros(buffer.shape, buffer.dtype), pieces)
    return running


def render_tiles(buffer, tile_lists, tile_numbers, triangle):
    tile_group = group_of()
    block_count = tile_lists.shape[0] // tile_group

    def render_one_block(pieces):
        piece_lists, piece_tiles = pieces
        gathered, live_mask, choose = block_inputs(buffer, piece_lists)
        return composite(gathered, live_mask, piece_tiles, triangle)

    rendered = lax.map(
        render_one_block,
        (
            tile_lists.reshape(block_count, tile_group, LIST_LEN),
            tile_numbers.reshape(block_count, tile_group),
        ),
    )
    return rendered.reshape(tile_lists.shape[0], 3, TILE_PIXELS)


def slot_group():
    return 512


def pick_slots(source, slots):
    width = slot_group()
    blocks = slots.shape[0] // width
    safe_ids = jnp.maximum(slots, 0).reshape(blocks, width)

    def pick_one_block(block_ids):
        return jnp.dot(
            source,
            selector(source.shape[1], block_ids, source.dtype),
            precision=lax.Precision.HIGHEST,
        )

    picked = lax.map(pick_one_block, safe_ids)
    return jnp.transpose(picked, (1, 0, 2)).reshape(source.shape[0], slots.shape[0])


def return_slots(values, slots, local_count):
    width = slot_group()
    blocks = slots.shape[0] // width
    live = (slots >= 0).astype(values.dtype)
    masked = jnp.transpose(
        (values * live[None, :]).reshape(values.shape[0], blocks, width), (1, 0, 2)
    )
    safe_ids = jnp.maximum(slots, 0).reshape(blocks, width)

    def return_one_block(running, pieces):
        block_values, block_ids = pieces
        choose = selector(local_count, block_ids, values.dtype)
        return (
            running
            + lax.dot_general(
                block_values, choose, (((1,), (1,)), ((), ())), precision=lax.Precision.HIGHEST
            ),
            None,
        )

    total, unused = lax.scan(
        return_one_block,
        jnp.zeros((values.shape[0], local_count), values.dtype),
        (masked, safe_ids),
    )
    return total


def shards(
    gauss_params,
    adam_first,
    adam_second,
    camera,
    send_first,
    send_second,
    lists_first,
    lists_second,
    tiles_first,
    tiles_second,
    targets,
):
    devices = lax.axis_size("dev")
    image_width = TILES_X * tile_edge * 1.0
    image_height = lists_first.shape[0] * devices // TILES_X * tile_edge * 1.0
    local_count = gauss_params.shape[1]
    triangle = (jnp.arange(LIST_LEN)[:, None] < jnp.arange(LIST_LEN)[None, :]).astype(
        gauss_params.dtype
    )
    slots_first = send_first[0]
    picked = pick_slots(gauss_params, slots_first)

    def view_first(chosen):
        return project(chosen, camera[0], image_width, image_height)

    arrived = lax.all_to_all(picked, "dev", split_axis=1, concat_axis=1, tiled=True)
    buffer, pullback = jax.vjp(view_first, arrived)
    splat_grads = train_tiles(buffer, lists_first, tiles_first, targets, triangle)
    slot_grads = lax.all_to_all(
        pullback(splat_grads)[0], "dev", split_axis=1, concat_axis=1, tiled=True
    )
    gradient = return_slots(slot_grads, slots_first, local_count)
    new_first = 0.9 * adam_first + 0.1 * gradient
    new_second = 0.999 * adam_second + 0.001 * gradient * gradient
    step_sizes = jnp.asarray(rate_values(), gauss_params.dtype)[:, None]
    new_params = gauss_params - step_sizes * (new_first / bias_first) / (
        jnp.sqrt(new_second / bias_second) + adam_epsilon
    )
    picked_next = pick_slots(new_params, send_second[0])
    buffer_next = project(
        lax.all_to_all(picked_next, "dev", split_axis=1, concat_axis=1, tiled=True),
        camera[1],
        image_width,
        image_height,
    )
    rendered_next = render_tiles(buffer_next, lists_second, tiles_second, triangle)
    return (new_params, new_first, new_second, rendered_next)


def solution(mesh):
    placed = (
        P(None, "dev"),
        P(None, "dev"),
        P(None, "dev"),
        P(),
        P("dev", None),
        P("dev", None),
        P("dev", None),
        P("dev", None),
        P("dev"),
        P("dev"),
        P("dev", None, None),
    )
    return jax.shard_map(
        shards,
        mesh=mesh,
        in_specs=placed,
        out_specs=(P(None, "dev"), P(None, "dev"), P(None, "dev"), P("dev", None, None)),
        check_vma=False,
    )
```

profile of v0, /device:TPU:0, one launch (start us, length us, event | category | flops | bytes accessed | tf_op | source)
XLA Modules:
  0.0 493.7 jit_solution(3253605575347814456)
XLA Ops:
  1.6 60.9 %while.60 = (s32[]{:T(128)}, f32[8,59,512]{2,1,0:T(8,128)S(1)}, s32[8,512]{1,0:T(8,128)S(1)}, f32[59,8192]{1,0:T(8,128)}, s32[]{:T(128)}) while((s32[]{:T(128)}, f32[8,59,512]{2,1,0:T(8,128)S(1)}, s32[8,512]{1,0:T(8,128)S(1)}, f32[59,8192]{1,0:T(8,128)}, s32[]{:T(128)}) %tuple.414), condition=%wide.region_1.2_spmd, body=%wide.region_0.1_spmd.sunk | while | flops 2973761536 | bytes 2070597 | solution.py:321
  1.6 7.6 %fusion.409 = f32[8,59,512]{2,1,0:T(8,128)S(1)} fusion(f32[8,59,512]{2,1,0:T(8,128)S(1)} %get-tuple-element.1000, s32[]{:T(128)} %get-tuple-element.999, f32[59,8192]{1,0:T(8,128)} %get-tuple-element.1007, s32[512]{0:T(512)S(1)} %bitcast.1571), kind=kOutput, calls=%fused_computation.6.clone.1 | convolution fusion | flops 2973761536 | bytes 2066436 | tf_op jit(solution)/shard_map/while/body/eval_jaxpr/dot_general | solution.py:315
  9.2 7.6 %fusion.409 = f32[8,59,512]{2,1,0:T(8,128)S(1)} fusion(f32[8,59,512]{2,1,0:T(8,128)S(1)} %get-tuple-element.1000, s32[]{:T(128)} %get-tuple-element.999, f32[59,8192]{1,0:T(8,128)} %get-tuple-element.1007, s32[512]{0:T(512)S(1)} %bitcast.1571), kind=kOutput, calls=%fused_computation.6.clone.1 | convolution fusion | flops 2973761536 | bytes 2066436 | tf_op jit(solution)/shard_map/while/body/eval_jaxpr/dot_general | solution.py:315
  16.9 7.6 %fusion.409 = f32[8,59,512]{2,1,0:T(8,128)S(1)} fusion(f32[8,59,512]{2,1,0:T(8,128)S(1)} %get-tuple-element.1000, s32[]{:T(128)} %get-tuple-element.999, f32[59,8192]{1,0:T(8,128)} %get-tuple-element.1007, s32[512]{0:T(512)S(1)} %bitcast.1571), kind=kOutput, calls=%fused_computation.6.clone.1 | convolution fusion | flops 2973761536 | bytes 2066436 | tf_op jit(solution)/shard_map/while/body/eval_jaxpr/dot_general | solution.py:315
  24.5 7.6 %fusion.409 = f32[8,59,512]{2,1,0:T(8,128)S(1)} fusion(f32[8,59,512]{2,1,0:T(8,128)S(1)} %get-tuple-element.1000, s32[]{:T(128)} %get-tuple-element.999, f32[59,8192]{1,0:T(8,128)} %get-tuple-element.1007, s32[512]{0:T(512)S(1)} %bitcast.1571), kind=kOutput, calls=%fused_computation.6.clone.1 | convolution fusion | flops 2973761536 | bytes 2066436 | tf_op jit(solution)/shard_map/while/body/eval_jaxpr/dot_general | solution.py:315
  32.1 7.6 %fusion.409 = f32[8,59,512]{2,1,0:T(8,128)S(1)} fusion(f32[8,59,512]{2,1,0:T(8,128)S(1)} %get-tuple-element.1000, s32[]{:T(128)} %get-tuple-element.999, f32[59,8192]{1,0:T(8,128)} %get-tuple-element.1007, s32[512]{0:T(512)S(1)} %bitcast.1571), kind=kOutput, calls=%fused_computation.6.clone.1 | convolution fusion | flops 2973761536 | bytes 2066436 | tf_op jit(solution)/shard_map/while/body/eval_jaxpr/dot_general | solution.py:315
  39.7 7.6 %fusion.409 = f32[8,59,512]{2,1,0:T(8,128)S(1)} fusion(f32[8,59,512]{2,1,0:T(8,128)S(1)} %get-tuple-element.1000, s32[]{:T(128)} %get-tuple-element.999, f32[59,8192]{1,0:T(8,128)} %get-tuple-element.1007, s32[512]{0:T(512)S(1)} %bitcast.1571), kind=kOutput, calls=%fused_computation.6.clone.1 | convolution fusion | flops 2973761536 | bytes 2066436 | tf_op jit(solution)/shard_map/while/body/eval_jaxpr/dot_general | solution.py:315
  47.3 7.6 %fusion.409 = f32[8,59,512]{2,1,0:T(8,128)S(1)} fusion(f32[8,59,512]{2,1,0:T(8,128)S(1)} %get-tuple-element.1000, s32[]{:T(128)} %get-tuple-element.999, f32[59,8192]{1,0:T(8,128)} %get-tuple-element.1007, s32[512]{0:T(512)S(1)} %bitcast.1571), kind=kOutput, calls=%fused_computation.6.clone.1 | convolution fusion | flops 2973761536 | bytes 2066436 | tf_op jit(solution)/shard_map/while/body/eval_jaxpr/dot_general | solution.py:315
  54.9 7.6 %fusion.409 = f32[8,59,512]{2,1,0:T(8,128)S(1)} fusion(f32[8,59,512]{2,1,0:T(8,128)S(1)} %get-tuple-element.1000, s32[]{:T(128)} %get-tuple-element.999, f32[59,8192]{1,0:T(8,128)} %get-tuple-element.1007, s32[512]{0:T(512)S(1)} %bitcast.1571), kind=kOutput, calls=%fused_computation.6.clone.1 | convolution fusion | flops 2973761536 | bytes 2066436 | tf_op jit(solution)/shard_map/while/body/eval_jaxpr/dot_general | solution.py:315
  98.4 7.6 %broadcast_multiply_fusion.3 = (f32[1,32,128]{2,1,0:T(8,128)S(1)}, f32[1,32,128]{2,1,0:T(8,128)S(1)}, f32[1,32,128]{2,1,0:T(8,128)S(1)}, f32[1,32,128]{2,1,0:T(8...) fusion(f32[]{:T(128)} %bitcast.25, ...), kind=kLoop, calls=%fused_computation.629 | loop fusion | flops 102400 | bytes 196668 | tf_op jit(solution)/shard_map/jvp()/mul | solution.py:156
  110.5 94.4 %while.64 = (s32[]{:T(128)}, f32[9,4096]{1,0:T(8,128)S(1)}, s32[4,8,128]{2,1,0:T(8,128)S(1)}, f32[9,4096]{1,0:T(8,128)S(1)}, s32[4,8]{1,0:T(4,128)S(1)}, /*index...) while((s32[]{:T(128)}, f32[9,4096]{1,0:T(8,128)S(1)}, ...), condition=%wide.region_10.11_spmd.clone.clone, body=%wide.region_3.10_spmd.clone.clone.sunk | while | flops 1775461632 | bytes 7651711 | solution.py:282
  232.2 26.1 %all-to-all-done.1 = f32[59,32,128]{2,0,1:T(8,128)S(1)} async-done(((f32[59,32,128]{2,0,1:T(8,128)}), f32[59,32,128]{2,0,1:T(8,128)S(1)}, u32[]{:S(2)}, u32[]{:S(2)}) %all-to-all-start.1) | async-done | bytes 966688 | tf_op jit(solution)/shard_map/all_to_all | solution.py:382
  259.1 86.1 %while.63 = (s32[]{:T(128)}, f32[59,8192]{1,0:T(8,128)}, f32[8,59,512]{2,0,1:T(8,128)S(1)}, s32[8,512]{1,0:T(8,128)S(1)}, s32[]{:T(128)}, /*index=5*/s32[]{:T(128)}) while((s32[]{:T(128)}, f32[59,8192]{1,0:T(8,128)}, f32[8,59,512]{2,0,1:T(8,128)S(1)}, s32[8,512]{1,0:T(8,128)S(1)}, s32[]{:T(128)}, /*index=5*/s32[]{:T(128)}) %tuple.432), condition=%wide.region_13.14_spmd.clone, body=%wide.region_12.13_spmd.clone.sunk | while | flops 2974728192 | bytes 4235351 | solution.py:345
  259.3 9.6 %fusion.421 = f32[59,8192]{1,0:T(8,128)} fusion(s32[512]{0:T(512)S(1)} %bitcast.1570, f32[59,8192]{1,0:T(8,128)} %get-tuple-element.1043, pred[]{:T(512)S(6)} %compare.133, f32[1,59,512]{2,0,1:T(1,128)S(1)} %constant_dynamic-slice_fusion.13), kind=kOutput, calls=%fused_computation.72.clone.1 | convolution fusion | flops 2974728192 | bytes 3989505 | tf_op jit(solution)/shard_map/while/body/eval_jaxpr/dot_general | solution.py:339
  269.0 10.8 %fusion.421 = f32[59,8192]{1,0:T(8,128)} fusion(s32[512]{0:T(512)S(1)} %bitcast.1570, f32[59,8192]{1,0:T(8,128)} %get-tuple-element.1043, pred[]{:T(512)S(6)} %compare.133, f32[1,59,512]{2,0,1:T(1,128)S(1)} %constant_dynamic-slice_fusion.13), kind=kOutput, calls=%fused_computation.72.clone.1 | convolution fusion | flops 2974728192 | bytes 3989505 | tf_op jit(solution)/shard_map/while/body/eval_jaxpr/dot_general | solution.py:339
  279.9 10.8 %fusion.421 = f32[59,8192]{1,0:T(8,128)} fusion(s32[512]{0:T(512)S(1)} %bitcast.1570, f32[59,8192]{1,0:T(8,128)} %get-tuple-element.1043, pred[]{:T(512)S(6)} %compare.133, f32[1,59,512]{2,0,1:T(1,128)S(1)} %constant_dynamic-slice_fusion.13), kind=kOutput, calls=%fused_computation.72.clone.1 | convolution fusion | flops 2974728192 | bytes 3989505 | tf_op jit(solution)/shard_map/while/body/eval_jaxpr/dot_general | solution.py:339
  290.8 10.8 %fusion.421 = f32[59,8192]{1,0:T(8,128)} fusion(s32[512]{0:T(512)S(1)} %bitcast.1570, f32[59,8192]{1,0:T(8,128)} %get-tuple-element.1043, pred[]{:T(512)S(6)} %compare.133, f32[1,59,512]{2,0,1:T(1,128)S(1)} %constant_dynamic-slice_fusion.13), kind=kOutput, calls=%fused_computation.72.clone.1 | convolution fusion | flops 2974728192 | bytes 3989505 | tf_op jit(solution)/shard_map/while/body/eval_jaxpr/dot_general | solution.py:339
  301.7 10.8 %fusion.421 = f32[59,8192]{1,0:T(8,128)} fusion(s32[512]{0:T(512)S(1)} %bitcast.1570, f32[59,8192]{1,0:T(8,128)} %get-tuple-element.1043, pred[]{:T(512)S(6)} %compare.133, f32[1,59,512]{2,0,1:T(1,128)S(1)} %constant_dynamic-slice_fusion.13), kind=kOutput, calls=%fused_computation.72.clone.1 | convolution fusion | flops 2974728192 | bytes 3989505 | tf_op jit(solution)/shard_map/while/body/eval_jaxpr/dot_general | solution.py:339
  312.7 10.8 %fusion.421 = f32[59,8192]{1,0:T(8,128)} fusion(s32[512]{0:T(512)S(1)} %bitcast.1570, f32[59,8192]{1,0:T(8,128)} %get-tuple-element.1043, pred[]{:T(512)S(6)} %compare.133, f32[1,59,512]{2,0,1:T(1,128)S(1)} %constant_dynamic-slice_fusion.13), kind=kOutput, calls=%fused_computation.72.clone.1 | convolution fusion | flops 2974728192 | bytes 3989505 | tf_op jit(solution)/shard_map/while/body/eval_jaxpr/dot_general | solution.py:339
  323.6 10.8 %fusion.421 = f32[59,8192]{1,0:T(8,128)} fusion(s32[512]{0:T(512)S(1)} %bitcast.1570, f32[59,8192]{1,0:T(8,128)} %get-tuple-element.1043, pred[]{:T(512)S(6)} %compare.133, f32[1,59,512]{2,0,1:T(1,128)S(1)} %constant_dynamic-slice_fusion.13), kind=kOutput, calls=%fused_computation.72.clone.1 | convolution fusion | flops 2974728192 | bytes 3989505 | tf_op jit(solution)/shard_map/while/body/eval_jaxpr/dot_general | solution.py:339
  334.5 10.8 %fusion.421 = f32[59,8192]{1,0:T(8,128)} fusion(s32[512]{0:T(512)S(1)} %bitcast.1570, f32[59,8192]{1,0:T(8,128)} %get-tuple-element.1043, pred[]{:T(512)S(6)} %compare.133, f32[1,59,512]{2,0,1:T(1,128)S(1)} %constant_dynamic-slice_fusion.13), kind=kOutput, calls=%fused_computation.72.clone.1 | convolution fusion | flops 2974728192 | bytes 3989505 | tf_op jit(solution)/shard_map/while/body/eval_jaxpr/dot_general | solution.py:339
  351.7 60.9 %while.61 = (s32[]{:T(128)}, f32[8,59,512]{2,1,0:T(8,128)S(1)}, s32[8,512]{1,0:T(8,128)S(1)}, f32[59,8192]{1,0:T(8,128)}, s32[]{:T(128)}) while((s32[]{:T(128)}, f32[8,59,512]{2,1,0:T(8,128)S(1)}, s32[8,512]{1,0:T(8,128)S(1)}, f32[59,8192]{1,0:T(8,128)}, s32[]{:T(128)}) %tuple.423), condition=%wide.region_15.16_spmd, body=%wide.region_14.15_spmd.sunk | while | flops 2973761536 | bytes 2070597 | solution.py:321
  351.8 7.6 %fusion.411 = f32[8,59,512]{2,1,0:T(8,128)S(1)} fusion(f32[8,59,512]{2,1,0:T(8,128)S(1)} %get-tuple-element.1060, s32[]{:T(128)} %get-tuple-element.1059, f32[59,8192]{1,0:T(8,128)} %get-tuple-element.1067, s32[512]{0:T(512)S(1)} %bitcast.1572), kind=kOutput, calls=%fused_computation.12.clone.1 | convolution fusion | flops 2973761536 | bytes 2066436 | tf_op jit(solution)/shard_map/while/body/eval_jaxpr/dot_general | solution.py:315
  359.4 7.6 %fusion.411 = f32[8,59,512]{2,1,0:T(8,128)S(1)} fusion(f32[8,59,512]{2,1,0:T(8,128)S(1)} %get-tuple-element.1060, s32[]{:T(128)} %get-tuple-element.1059, f32[59,8192]{1,0:T(8,128)} %get-tuple-element.1067, s32[512]{0:T(512)S(1)} %bitcast.1572), kind=kOutput, calls=%fused_computation.12.clone.1 | convolution fusion | flops 2973761536 | bytes 2066436 | tf_op jit(solution)/shard_map/while/body/eval_jaxpr/dot_general | solution.py:315
  367.0 7.6 %fusion.411 = f32[8,59,512]{2,1,0:T(8,128)S(1)} fusion(f32[8,59,512]{2,1,0:T(8,128)S(1)} %get-tuple-element.1060, s32[]{:T(128)} %get-tuple-element.1059, f32[59,8192]{1,0:T(8,128)} %get-tuple-element.1067, s32[512]{0:T(512)S(1)} %bitcast.1572), kind=kOutput, calls=%fused_computation.12.clone.1 | convolution fusion | flops 2973761536 | bytes 2066436 | tf_op jit(solution)/shard_map/while/body/eval_jaxpr/dot_general | solution.py:315
  374.6 7.6 %fusion.411 = f32[8,59,512]{2,1,0:T(8,128)S(1)} fusion(f32[8,59,512]{2,1,0:T(8,128)S(1)} %get-tuple-element.1060, s32[]{:T(128)} %get-tuple-element.1059, f32[59,8192]{1,0:T(8,128)} %get-tuple-element.1067, s32[512]{0:T(512)S(1)} %bitcast.1572), kind=kOutput, calls=%fused_computation.12.clone.1 | convolution fusion | flops 2973761536 | bytes 2066436 | tf_op jit(solution)/shard_map/while/body/eval_jaxpr/dot_general | solution.py:315
  382.2 7.6 %fusion.411 = f32[8,59,512]{2,1,0:T(8,128)S(1)} fusion(f32[8,59,512]{2,1,0:T(8,128)S(1)} %get-tuple-element.1060, s32[]{:T(128)} %get-tuple-element.1059, f32[59,8192]{1,0:T(8,128)} %get-tuple-element.1067, s32[512]{0:T(512)S(1)} %bitcast.1572), kind=kOutput, calls=%fused_computation.12.clone.1 | convolution fusion | flops 2973761536 | bytes 2066436 | tf_op jit(solution)/shard_map/while/body/eval_jaxpr/dot_general | solution.py:315
  389.8 7.6 %fusion.411 = f32[8,59,512]{2,1,0:T(8,128)S(1)} fusion(f32[8,59,512]{2,1,0:T(8,128)S(1)} %get-tuple-element.1060, s32[]{:T(128)} %get-tuple-element.1059, f32[59,8192]{1,0:T(8,128)} %get-tuple-element.1067, s32[512]{0:T(512)S(1)} %bitcast.1572), kind=kOutput, calls=%fused_computation.12.clone.1 | convolution fusion | flops 2973761536 | bytes 2066436 | tf_op jit(solution)/shard_map/while/body/eval_jaxpr/dot_general | solution.py:315
  397.5 7.6 %fusion.411 = f32[8,59,512]{2,1,0:T(8,128)S(1)} fusion(f32[8,59,512]{2,1,0:T(8,128)S(1)} %get-tuple-element.1060, s32[]{:T(128)} %get-tuple-element.1059, f32[59,8192]{1,0:T(8,128)} %get-tuple-element.1067, s32[512]{0:T(512)S(1)} %bitcast.1572), kind=kOutput, calls=%fused_computation.12.clone.1 | convolution fusion | flops 2973761536 | bytes 2066436 | tf_op jit(solution)/shard_map/while/body/eval_jaxpr/dot_general | solution.py:315
  405.1 7.6 %fusion.411 = f32[8,59,512]{2,1,0:T(8,128)S(1)} fusion(f32[8,59,512]{2,1,0:T(8,128)S(1)} %get-tuple-element.1060, s32[]{:T(128)} %get-tuple-element.1059, f32[59,8192]{1,0:T(8,128)} %get-tuple-element.1067, s32[512]{0:T(512)S(1)} %bitcast.1572), kind=kOutput, calls=%fused_computation.12.clone.1 | convolution fusion | flops 2973761536 | bytes 2066436 | tf_op jit(solution)/shard_map/while/body/eval_jaxpr/dot_general | solution.py:315
  445.0 7.6 %broadcast_multiply_fusion.1 = (f32[1,32,128]{2,1,0:T(8,128)S(1)}, f32[1,32,128]{2,1,0:T(8,128)S(1)}, f32[1,32,128]{2,1,0:T(8,128)S(1)}, f32[1,32,128]{2,1,0:T(8...) fusion(f32[]{:T(128)} %bitcast.132, ...), kind=kLoop, calls=%fused_computation.627 | loop fusion | flops 98304 | bytes 180284 | tf_op jit(solution)/shard_map/mul | solution.py:156
  457.4 36.0 %while.62 = (s32[]{:T(128)}, f32[4,8,3,256]{3,1,0,2:T(8,128)}, s32[4,8,128]{2,1,0:T(8,128)S(1)}, f32[9,4096]{1,0:T(8,128)S(1)}, s32[4,8]{1,0:T(4,128)S(1)}, /*index=5*/s32[]{:T(128)}) while((s32[]{:T(128)}, f32[4,8,3,256]{3,1,0,2:T(8,128)}, s32[4,8,128]{2,1,0:T(8,128)S(1)}, f32[9,4096]{1,0:T(8,128)S(1)}, s32[4,8]{1,0:T(4,128)S(1)}, ...), condition=%wide.region_18.19_spmd.clone, body=%wide.region_17.18_spmd.clone.sunk | while | flops 876660928 | bytes 2507605 | solution.py:295
  (287 shorter events, 196.2 us)
Async XLA Ops:
  63.1 8.9 %copy-start.5 = (f32[2,6]{1,0:T(2,128)S(1)}, f32[2,6]{1,0:T(2,128)}, u32[]{:S(2)}) copy-start(f32[2,6]{1,0:T(2,128)} %param.25) | copy-start | bytes 148
  63.2 14.1 %copy-start.10 = (f32[1,3]{1,0:T(1,128)S(1)}, f32[1,3]{1,0:T(1,128)}, u32[]{:S(2)}) copy-start(f32[1,3]{1,0:T(1,128)} %constant.324.clone.1) | copy-start | bytes 40
  63.2 14.1 %copy-start.11 = (f32[1,3]{1,0:T(1,128)S(1)}, f32[1,3]{1,0:T(1,128)}, u32[]{:S(2)}) copy-start(f32[1,3]{1,0:T(1,128)} %constant.325.clone.1) | copy-start | bytes 40
  63.2 14.2 %copy-start.6 = (f32[1,3]{1,0:T(1,128)S(1)}, f32[1,3]{1,0:T(1,128)}, u32[]{:S(2)}) copy-start(f32[1,3]{1,0:T(1,128)} %constant.323.clone.1) | copy-start | bytes 40
  63.2 34.1 %copy-start.3 = (f32[32,3,256]{2,0,1:T(8,128)S(1)}, f32[32,3,256]{2,0,1:T(8,128)}, u32[]{:S(2)}) copy-start(f32[32,3,256]{2,0,1:T(8,128)} %param.32) | copy-start | bytes 294916
  63.2 34.1 %copy-start.8 = (s32[32]{0:T(128)S(1)}, s32[32]{0:T(128)}, u32[]{:S(2)}) copy-start(s32[32]{0:T(128)} %param.30) | copy-start | bytes 388
  64.8 33.5 %all-to-all-start = ((f32[59,32,128]{2,0,1:T(8,128)}), f32[59,32,128]{2,0,1:T(8,128)S(1)}, u32[]{:S(2)}, u32[]{:S(2)}) async-start(f32[59,32,128]{2,0,1:T(8,128)} %copy.60), calls=%async_computation | async-start | bytes 2097152 | tf_op jit(solution)/shard_map/all_to_all | solution.py:379
  92.2 18.3 %copy-start.1 = (s32[32,128]{1,0:T(8,128)S(1)}, s32[32,128]{1,0:T(8,128)}, u32[]{:S(2)}) copy-start(s32[32,128]{1,0:T(8,128)} %param.28) | copy-start | bytes 49156
  225.4 6.7 %copy-start.4 = (s32[1,4096]{1,0:T(1,128)S(1)}, s32[1,4096]{1,0:T(1,128)}, u32[]{:S(2)}) copy-start(s32[1,4096]{1,0:T(1,128)} %param.26) | copy-start | bytes 49156
  226.9 31.4 %all-to-all-start.1 = ((f32[59,32,128]{2,0,1:T(8,128)}), f32[59,32,128]{2,0,1:T(8,128)S(1)}, u32[]{:S(2)}, u32[]{:S(2)}) async-start(f32[59,32,128]{2,0,1:T(8,128)} %copy.66), calls=%async_computation.1 | async-start | bytes 2097152 | tf_op jit(solution)/shard_map/all_to_all | solution.py:382
  259.1 86.2 %copy-start = (f32[59,8192]{1,0:T(8,128)S(1)}, f32[59,8192]{1,0:T(8,128)}, u32[]{:S(2)}) copy-start(f32[59,8192]{1,0:T(8,128)} %get-tuple-element.1090) | copy-start | bytes 5799940
  259.1 86.2 %copy-start.7 = (f32[59]{0:T(128)S(1)}, f32[59]{0:T(128)}, u32[]{:S(2)}) copy-start(f32[59]{0:T(128)} %constant.528) | copy-start | bytes 712
  413.3 29.9 %copy-start.9 = (s32[32]{0:T(128)S(1)}, s32[32]{0:T(128)}, u32[]{:S(2)}) copy-start(s32[32]{0:T(128)} %param.31) | copy-start | bytes 388
  414.8 30.0 %all-to-all-start.2 = ((f32[59,32,128]{2,0,1:T(8,128)}), f32[59,32,128]{2,0,1:T(8,128)S(1)}, u32[]{:S(2)}, u32[]{:S(2)}) async-start(f32[59,32,128]{2,0,1:T(8,128)} %copy.70), calls=%async_computation.2 | async-start | bytes 2097152 | tf_op jit(solution)/shard_map/all_to_all | solution.py:394
  418.7 38.7 %copy-start.2 = (s32[32,128]{1,0:T(8,128)S(1)}, s32[32,128]{1,0:T(8,128)}, u32[]{:S(2)}) copy-start(s32[32,128]{1,0:T(8,128)} %param.29) | copy-start | bytes 49156
where the time goes:
time: 503 us; the launch traced here: 494 us
  matrix products  332 us (66%)
  other arithmetic  53.5 us (11%)
  between operations  48.2 us (10%)
  waiting for transfers between devices  28.5 us (6%)
  starting transfers between devices  16.3 us (3%)
  local copies, waits for them, and re-layouts  13.9 us (3%)
    dot_general x16, matrix products, pick_one_block(): jnp.dot(source, selector(source.shape[1], block_ids, source.dtype), preci...  121 us
    dot_general x8, matrix products, return_one_block(): lax.dot_general(block_values, choose, (((1,), (1,)), ((), ())), precision...  85.1 us
    dot_general x8, matrix products, block_inputs(): jnp.dot(buffer, choose, precision=lax.Precision.HIGHEST)  41.3 us
    dot_general x4, matrix products, train_one_block(): lax.dot_general(splat_grad, choose, (((1,), (1,)), ((), ())), precision=l...  29.6 us
    dot_general x12, matrix products, composite(): jnp.einsum('bpj,ji->bpi', log_clear, triangle, precision=lax.Precision.HI...  29.2 us
    all_to_all x1, waiting for transfers between devices, shards(): lax.all_to_all(pullback(splat_grads)[0], 'dev', split_axis=1, concat_axis...  26.1 us
    dot_general x16, matrix products, composite(): jnp.einsum('bpi,cbi->bcp', weight, gathered[6:9], precision=lax.Precision...  24.5 us
    mul x2, other arithmetic, project(): -focal_length * viewed[1] * inverse_depth * inverse_depth  15.2 us
  transfers between devices with their start and end apart: 3, of which 3 were waited for; matrix products, arithmetic and copies ran while one was open for 1% of the time, Pallas kernels for 0%

commit v1 on v0

--- a/solution.py
+++ b/solution.py
@@ -33,6 +33,12 @@
 )
 
 
+def exchange_blocks(shard, axis, split, join):
+    shards = jnp.split(shard, lax.axis_size(axis), axis=split)
+    incoming = lax.all_to_all(jnp.stack(shards), axis, 0, 0)
+    return jnp.concatenate(incoming, axis=join)
+
+
 def rate_values():
     values = np.full((59,), 0.000125)
     values[0:3] = 0.00016
@@ -379,9 +385,7 @@
     arrived = lax.all_to_all(picked, "dev", split_axis=1, concat_axis=1, tiled=True)
     buffer, pullback = jax.vjp(view_first, arrived)
     splat_grads = train_tiles(buffer, lists_first, tiles_first, targets, triangle)
-    slot_grads = lax.all_to_all(
-        pullback(splat_grads)[0], "dev", split_axis=1, concat_axis=1, tiled=True
-    )
+    slot_grads = exchange_blocks(pullback(splat_grads)[0], "dev", 1, 1)
     gradient = return_slots(slot_grads, slots_first, local_count)
     new_first = 0.9 * adam_first + 0.1 * gradient
     new_second = 0.999 * adam_second + 0.001 * gradient * gradient

time: 503 us -> 534 us (1.062)
  local copies, waits for them, and re-layouts: 13.9 us -> 31.9 us
  loops' own time: 1.62 us -> 14.4 us
    unnamed x26 -> x56, local copies, waits for them, and re-layouts: 0.34 us -> 19.3 us
    another operation x1, loops' own time: 0.95 us -> 13.8 us  [train_tiles(): lax.scan(train_one_block, jnp.zeros(buffer.shape, buffer.dtype), pieces)]
where the time goes in v1:
time: 534 us; the launch traced here: 525 us
  matrix products  332 us (62%)
  other arithmetic  53.5 us (10%)
  between operations  48.3 us (9%)
  local copies, waits for them, and re-layouts  31.9 us (6%)
  waiting for transfers between devices  28.5 us (5%)
  starting transfers between devices  16.1 us (3%)
  loops' own time  14.4 us (3%)
    dot_general x16, matrix products, pick_one_block(): jnp.dot(source, selector(source.shape[1], block_ids, source.dtype), preci...  121 us
    dot_general x8, matrix products, return_one_block(): lax.dot_general(block_values, choose, (((1,), (1,)), ((), ())), precision...  85.1 us
    dot_general x8, matrix products, block_inputs(): jnp.dot(buffer, choose, precision=lax.Precision.HIGHEST)  41.3 us
    dot_general x4, matrix products, train_one_block(): lax.dot_general(splat_grad, choose, (((1,), (1,)), ((), ())), precision=l...  29.6 us
    dot_general x12, matrix products, composite(): jnp.einsum('bpj,ji->bpi', log_clear, triangle, precision=lax.Precision.HI...  29.2 us
    all_to_all x1, waiting for transfers between devices, exchange_blocks(): incoming = lax.all_to_all(jnp.stack(shards), axis, 0, 0)  26.1 us
    dot_general x16, matrix products, composite(): jnp.einsum('bpi,cbi->bcp', weight, gathered[6:9], precision=lax.Precision...  24.5 us
    unnamed x56, local copies, waits for them, and re-layouts  19.3 us
  transfers between devices with their start and end apart: 3, of which 3 were waited for; matrix products, arithmetic and copies ran while one was open for 1% of the time, Pallas kernels for 0%

profile of v1, /device:TPU:0, one launch (start us, length us, event | category | flops | bytes accessed | tf_op | source)
XLA Modules:
  0.0 524.5 jit_solution(9010909578788632335)
XLA Ops:
  1.6 60.9 %while.60 = (s32[]{:T(128)}, f32[8,59,512]{2,1,0:T(8,128)S(1)}, s32[8,512]{1,0:T(8,128)S(1)}, f32[59,8192]{1,0:T(8,128)}, s32[]{:T(128)}) while((s32[]{:T(128)}, f32[8,59,512]{2,1,0:T(8,128)S(1)}, s32[8,512]{1,0:T(8,128)S(1)}, f32[59,8192]{1,0:T(8,128)}, s32[]{:T(128)}) %tuple.413), condition=%wide.region_1.2_spmd, body=%wide.region_0.1_spmd.sunk | while | flops 2973761536 | bytes 2070597 | solution.py:327
  1.6 7.6 %fusion.409 = f32[8,59,512]{2,1,0:T(8,128)S(1)} fusion(f32[8,59,512]{2,1,0:T(8,128)S(1)} %get-tuple-element.996, s32[]{:T(128)} %get-tuple-element.995, f32[59,8192]{1,0:T(8,128)} %get-tuple-element.1003, s32[512]{0:T(512)S(1)} %bitcast.1696), kind=kOutput, calls=%fused_computation.6.clone.1 | convolution fusion | flops 2973761536 | bytes 2066436 | tf_op jit(solution)/shard_map/while/body/eval_jaxpr/dot_general | solution.py:321
  9.2 7.6 %fusion.409 = f32[8,59,512]{2,1,0:T(8,128)S(1)} fusion(f32[8,59,512]{2,1,0:T(8,128)S(1)} %get-tuple-element.996, s32[]{:T(128)} %get-tuple-element.995, f32[59,8192]{1,0:T(8,128)} %get-tuple-element.1003, s32[512]{0:T(512)S(1)} %bitcast.1696), kind=kOutput, calls=%fused_computation.6.clone.1 | convolution fusion | flops 2973761536 | bytes 2066436 | tf_op jit(solution)/shard_map/while/body/eval_jaxpr/dot_general | solution.py:321
  16.9 7.6 %fusion.409 = f32[8,59,512]{2,1,0:T(8,128)S(1)} fusion(f32[8,59,512]{2,1,0:T(8,128)S(1)} %get-tuple-element.996, s32[]{:T(128)} %get-tuple-element.995, f32[59,8192]{1,0:T(8,128)} %get-tuple-element.1003, s32[512]{0:T(512)S(1)} %bitcast.1696), kind=kOutput, calls=%fused_computation.6.clone.1 | convolution fusion | flops 2973761536 | bytes 2066436 | tf_op jit(solution)/shard_map/while/body/eval_jaxpr/dot_general | solution.py:321
  24.5 7.6 %fusion.409 = f32[8,59,512]{2,1,0:T(8,128)S(1)} fusion(f32[8,59,512]{2,1,0:T(8,128)S(1)} %get-tuple-element.996, s32[]{:T(128)} %get-tuple-element.995, f32[59,8192]{1,0:T(8,128)} %get-tuple-element.1003, s32[512]{0:T(512)S(1)} %bitcast.1696), kind=kOutput, calls=%fused_computation.6.clone.1 | convolution fusion | flops 2973761536 | bytes 2066436 | tf_op jit(solution)/shard_map/while/body/eval_jaxpr/dot_general | solution.py:321
  32.1 7.6 %fusion.409 = f32[8,59,512]{2,1,0:T(8,128)S(1)} fusion(f32[8,59,512]{2,1,0:T(8,128)S(1)} %get-tuple-element.996, s32[]{:T(128)} %get-tuple-element.995, f32[59,8192]{1,0:T(8,128)} %get-tuple-element.1003, s32[512]{0:T(512)S(1)} %bitcast.1696), kind=kOutput, calls=%fused_computation.6.clone.1 | convolution fusion | flops 2973761536 | bytes 2066436 | tf_op jit(solution)/shard_map/while/body/eval_jaxpr/dot_general | solution.py:321
  39.7 7.6 %fusion.409 = f32[8,59,512]{2,1,0:T(8,128)S(1)} fusion(f32[8,59,512]{2,1,0:T(8,128)S(1)} %get-tuple-element.996, s32[]{:T(128)} %get-tuple-element.995, f32[59,8192]{1,0:T(8,128)} %get-tuple-element.1003, s32[512]{0:T(512)S(1)} %bitcast.1696), kind=kOutput, calls=%fused_computation.6.clone.1 | convolution fusion | flops 2973761536 | bytes 2066436 | tf_op jit(solution)/shard_map/while/body/eval_jaxpr/dot_general | solution.py:321
  47.3 7.6 %fusion.409 = f32[8,59,512]{2,1,0:T(8,128)S(1)} fusion(f32[8,59,512]{2,1,0:T(8,128)S(1)} %get-tuple-element.996, s32[]{:T(128)} %get-tuple-element.995, f32[59,8192]{1,0:T(8,128)} %get-tuple-element.1003, s32[512]{0:T(512)S(1)} %bitcast.1696), kind=kOutput, calls=%fused_computation.6.clone.1 | convolution fusion | flops 2973761536 | bytes 2066436 | tf_op jit(solution)/shard_map/while/body/eval_jaxpr/dot_general | solution.py:321
  54.9 7.6 %fusion.409 = f32[8,59,512]{2,1,0:T(8,128)S(1)} fusion(f32[8,59,512]{2,1,0:T(8,128)S(1)} %get-tuple-element.996, s32[]{:T(128)} %get-tuple-element.995, f32[59,8192]{1,0:T(8,128)} %get-tuple-element.1003, s32[512]{0:T(512)S(1)} %bitcast.1696), kind=kOutput, calls=%fused_computation.6.clone.1 | convolution fusion | flops 2973761536 | bytes 2066436 | tf_op jit(solution)/shard_map/while/body/eval_jaxpr/dot_general | solution.py:321
  98.4 7.6 %broadcast_multiply_fusion.3 = (f32[1,32,128]{2,1,0:T(8,128)S(1)}, f32[1,32,128]{2,1,0:T(8,128)S(1)}, f32[1,32,128]{2,1,0:T(8,128)S(1)}, f32[1,32,128]{2,1,0:T(8...) fusion(f32[]{:T(128)} %bitcast.25, ...), kind=kLoop, calls=%fused_computation.693 | loop fusion | flops 102400 | bytes 196668 | tf_op jit(solution)/shard_map/jvp()/mul | solution.py:162
  110.5 107.2 %while.64 = (s32[]{:T(128)}, f32[9,4096]{1,0:T(8,128)S(1)}, s32[4,8,128]{2,1,0:T(8,128)S(1)}, f32[9,4096]{1,0:T(8,128)S(1)}, s32[4,8]{1,0:T(4,128)S(1)}, /*index...) while((s32[]{:T(128)}, f32[9,4096]{1,0:T(8,128)S(1)}, ...), condition=%wide.region_10.11_spmd.clone.clone, body=%wide.region_3.10_spmd.clone.clone.sunk | while | flops 1775461632 | bytes 7651711 | solution.py:288
  262.9 26.1 %all-to-all-done.1 = f32[32,59,128]{2,1,0:T(8,128)S(1)} async-done(((f32[32,59,128]{2,1,0:T(8,128)}), f32[32,59,128]{2,1,0:T(8,128)S(1)}, u32[]{:S(2)}, u32[]{:S(2)}) %all-to-all-start.1) | async-done | bytes 966688 | tf_op jit(solution)/shard_map/all_to_all | solution.py:38
  289.9 86.1 %while.63 = (s32[]{:T(128)}, f32[59,8192]{1,0:T(8,128)}, f32[8,59,512]{2,0,1:T(8,128)S(1)}, s32[8,512]{1,0:T(8,128)S(1)}, s32[]{:T(128)}, /*index=5*/s32[]{:T(128)}) while((s32[]{:T(128)}, f32[59,8192]{1,0:T(8,128)}, f32[8,59,512]{2,0,1:T(8,128)S(1)}, s32[8,512]{1,0:T(8,128)S(1)}, s32[]{:T(128)}, /*index=5*/s32[]{:T(128)}) %tuple.431), condition=%wide.region_13.14_spmd.clone, body=%wide.region_12.13_spmd.clone.sunk | while | flops 2974728192 | bytes 4235351 | solution.py:351
  290.0 9.6 %fusion.421 = f32[59,8192]{1,0:T(8,128)} fusion(s32[512]{0:T(512)S(1)} %bitcast.1695, f32[59,8192]{1,0:T(8,128)} %get-tuple-element.1039, pred[]{:T(512)S(6)} %compare.133, f32[1,59,512]{2,0,1:T(1,128)S(1)} %constant_dynamic-slice_fusion.13), kind=kOutput, calls=%fused_computation.72.clone.1 | convolution fusion | flops 2974728192 | bytes 3989505 | tf_op jit(solution)/shard_map/while/body/eval_jaxpr/dot_general | solution.py:345
  299.7 10.8 %fusion.421 = f32[59,8192]{1,0:T(8,128)} fusion(s32[512]{0:T(512)S(1)} %bitcast.1695, f32[59,8192]{1,0:T(8,128)} %get-tuple-element.1039, pred[]{:T(512)S(6)} %compare.133, f32[1,59,512]{2,0,1:T(1,128)S(1)} %constant_dynamic-slice_fusion.13), kind=kOutput, calls=%fused_computation.72.clone.1 | convolution fusion | flops 2974728192 | bytes 3989505 | tf_op jit(solution)/shard_map/while/body/eval_jaxpr/dot_general | solution.py:345
  310.6 10.8 %fusion.421 = f32[59,8192]{1,0:T(8,128)} fusion(s32[512]{0:T(512)S(1)} %bitcast.1695, f32[59,8192]{1,0:T(8,128)} %get-tuple-element.1039, pred[]{:T(512)S(6)} %compare.133, f32[1,59,512]{2,0,1:T(1,128)S(1)} %constant_dynamic-slice_fusion.13), kind=kOutput, calls=%fused_computation.72.clone.1 | convolution fusion | flops 2974728192 | bytes 3989505 | tf_op jit(solution)/shard_map/while/body/eval_jaxpr/dot_general | solution.py:345
  321.5 10.8 %fusion.421 = f32[59,8192]{1,0:T(8,128)} fusion(s32[512]{0:T(512)S(1)} %bitcast.1695, f32[59,8192]{1,0:T(8,128)} %get-tuple-element.1039, pred[]{:T(512)S(6)} %compare.133, f32[1,59,512]{2,0,1:T(1,128)S(1)} %constant_dynamic-slice_fusion.13), kind=kOutput, calls=%fused_computation.72.clone.1 | convolution fusion | flops 2974728192 | bytes 3989505 | tf_op jit(solution)/shard_map/while/body/eval_jaxpr/dot_general | solution.py:345
  332.5 10.8 %fusion.421 = f32[59,8192]{1,0:T(8,128)} fusion(s32[512]{0:T(512)S(1)} %bitcast.1695, f32[59,8192]{1,0:T(8,128)} %get-tuple-element.1039, pred[]{:T(512)S(6)} %compare.133, f32[1,59,512]{2,0,1:T(1,128)S(1)} %constant_dynamic-slice_fusion.13), kind=kOutput, calls=%fused_computation.72.clone.1 | convolution fusion | flops 2974728192 | bytes 3989505 | tf_op jit(solution)/shard_map/while/body/eval_jaxpr/dot_general | solution.py:345
  343.4 10.8 %fusion.421 = f32[59,8192]{1,0:T(8,128)} fusion(s32[512]{0:T(512)S(1)} %bitcast.1695, f32[59,8192]{1,0:T(8,128)} %get-tuple-element.1039, pred[]{:T(512)S(6)} %compare.133, f32[1,59,512]{2,0,1:T(1,128)S(1)} %constant_dynamic-slice_fusion.13), kind=kOutput, calls=%fused_computation.72.clone.1 | convolution fusion | flops 2974728192 | bytes 3989505 | tf_op jit(solution)/shard_map/while/body/eval_jaxpr/dot_general | solution.py:345
  354.3 10.8 %fusion.421 = f32[59,8192]{1,0:T(8,128)} fusion(s32[512]{0:T(512)S(1)} %bitcast.1695, f32[59,8192]{1,0:T(8,128)} %get-tuple-element.1039, pred[]{:T(512)S(6)} %compare.133, f32[1,59,512]{2,0,1:T(1,128)S(1)} %constant_dynamic-slice_fusion.13), kind=kOutput, calls=%fused_computation.72.clone.1 | convolution fusion | flops 2974728192 | bytes 3989505 | tf_op jit(solution)/shard_map/while/body/eval_jaxpr/dot_general | solution.py:345
  365.2 10.8 %fusion.421 = f32[59,8192]{1,0:T(8,128)} fusion(s32[512]{0:T(512)S(1)} %bitcast.1695, f32[59,8192]{1,0:T(8,128)} %get-tuple-element.1039, pred[]{:T(512)S(6)} %compare.133, f32[1,59,512]{2,0,1:T(1,128)S(1)} %constant_dynamic-slice_fusion.13), kind=kOutput, calls=%fused_computation.72.clone.1 | convolution fusion | flops 2974728192 | bytes 3989505 | tf_op jit(solution)/shard_map/while/body/eval_jaxpr/dot_general | solution.py:345
  382.5 60.9 %while.61 = (s32[]{:T(128)}, f32[8,59,512]{2,1,0:T(8,128)S(1)}, s32[8,512]{1,0:T(8,128)S(1)}, f32[59,8192]{1,0:T(8,128)}, s32[]{:T(128)}) while((s32[]{:T(128)}, f32[8,59,512]{2,1,0:T(8,128)S(1)}, s32[8,512]{1,0:T(8,128)S(1)}, f32[59,8192]{1,0:T(8,128)}, s32[]{:T(128)}) %tuple.422), condition=%wide.region_15.16_spmd, body=%wide.region_14.15_spmd.sunk | while | flops 2973761536 | bytes 2070597 | solution.py:327
  382.5 7.6 %fusion.411 = f32[8,59,512]{2,1,0:T(8,128)S(1)} fusion(f32[8,59,512]{2,1,0:T(8,128)S(1)} %get-tuple-element.1056, s32[]{:T(128)} %get-tuple-element.1055, f32[59,8192]{1,0:T(8,128)} %get-tuple-element.1063, s32[512]{0:T(512)S(1)} %bitcast.1697), kind=kOutput, calls=%fused_computation.12.clone.1 | convolution fusion | flops 2973761536 | bytes 2066436 | tf_op jit(solution)/shard_map/while/body/eval_jaxpr/dot_general | solution.py:321
  390.1 7.6 %fusion.411 = f32[8,59,512]{2,1,0:T(8,128)S(1)} fusion(f32[8,59,512]{2,1,0:T(8,128)S(1)} %get-tuple-element.1056, s32[]{:T(128)} %get-tuple-element.1055, f32[59,8192]{1,0:T(8,128)} %get-tuple-element.1063, s32[512]{0:T(512)S(1)} %bitcast.1697), kind=kOutput, calls=%fused_computation.12.clone.1 | convolution fusion | flops 2973761536 | bytes 2066436 | tf_op jit(solution)/shard_map/while/body/eval_jaxpr/dot_general | solution.py:321
  397.7 7.6 %fusion.411 = f32[8,59,512]{2,1,0:T(8,128)S(1)} fusion(f32[8,59,512]{2,1,0:T(8,128)S(1)} %get-tuple-element.1056, s32[]{:T(128)} %get-tuple-element.1055, f32[59,8192]{1,0:T(8,128)} %get-tuple-element.1063, s32[512]{0:T(512)S(1)} %bitcast.1697), kind=kOutput, calls=%fused_computation.12.clone.1 | convolution fusion | flops 2973761536 | bytes 2066436 | tf_op jit(solution)/shard_map/while/body/eval_jaxpr/dot_general | solution.py:321
  405.3 7.6 %fusion.411 = f32[8,59,512]{2,1,0:T(8,128)S(1)} fusion(f32[8,59,512]{2,1,0:T(8,128)S(1)} %get-tuple-element.1056, s32[]{:T(128)} %get-tuple-element.1055, f32[59,8192]{1,0:T(8,128)} %get-tuple-element.1063, s32[512]{0:T(512)S(1)} %bitcast.1697), kind=kOutput, calls=%fused_computation.12.clone.1 | convolution fusion | flops 2973761536 | bytes 2066436 | tf_op jit(solution)/shard_map/while/body/eval_jaxpr/dot_general | solution.py:321
  412.9 7.6 %fusion.411 = f32[8,59,512]{2,1,0:T(8,128)S(1)} fusion(f32[8,59,512]{2,1,0:T(8,128)S(1)} %get-tuple-element.1056, s32[]{:T(128)} %get-tuple-element.1055, f32[59,8192]{1,0:T(8,128)} %get-tuple-element.1063, s32[512]{0:T(512)S(1)} %bitcast.1697), kind=kOutput, calls=%fused_computation.12.clone.1 | convolution fusion | flops 2973761536 | bytes 2066436 | tf_op jit(solution)/shard_map/while/body/eval_jaxpr/dot_general | solution.py:321
  420.5 7.6 %fusion.411 = f32[8,59,512]{2,1,0:T(8,128)S(1)} fusion(f32[8,59,512]{2,1,0:T(8,128)S(1)} %get-tuple-element.1056, s32[]{:T(128)} %get-tuple-element.1055, f32[59,8192]{1,0:T(8,128)} %get-tuple-element.1063, s32[512]{0:T(512)S(1)} %bitcast.1697), kind=kOutput, calls=%fused_computation.12.clone.1 | convolution fusion | flops 2973761536 | bytes 2066436 | tf_op jit(solution)/shard_map/while/body/eval_jaxpr/dot_general | solution.py:321
  428.2 7.6 %fusion.411 = f32[8,59,512]{2,1,0:T(8,128)S(1)} fusion(f32[8,59,512]{2,1,0:T(8,128)S(1)} %get-tuple-element.1056, s32[]{:T(128)} %get-tuple-element.1055, f32[59,8192]{1,0:T(8,128)} %get-tuple-element.1063, s32[512]{0:T(512)S(1)} %bitcast.1697), kind=kOutput, calls=%fused_computation.12.clone.1 | convolution fusion | flops 2973761536 | bytes 2066436 | tf_op jit(solution)/shard_map/while/body/eval_jaxpr/dot_general | solution.py:321
  435.8 7.6 %fusion.411 = f32[8,59,512]{2,1,0:T(8,128)S(1)} fusion(f32[8,59,512]{2,1,0:T(8,128)S(1)} %get-tuple-element.1056, s32[]{:T(128)} %get-tuple-element.1055, f32[59,8192]{1,0:T(8,128)} %get-tuple-element.1063, s32[512]{0:T(512)S(1)} %bitcast.1697), kind=kOutput, calls=%fused_computation.12.clone.1 | convolution fusion | flops 2973761536 | bytes 2066436 | tf_op jit(solution)/shard_map/while/body/eval_jaxpr/dot_general | solution.py:321
  475.7 7.6 %broadcast_multiply_fusion.1 = (f32[1,32,128]{2,1,0:T(8,128)S(1)}, f32[1,32,128]{2,1,0:T(8,128)S(1)}, f32[1,32,128]{2,1,0:T(8,128)S(1)}, f32[1,32,128]{2,1,0:T(8...) fusion(f32[]{:T(128)} %bitcast.165, ...), kind=kLoop, calls=%fused_computation.691 | loop fusion | flops 98304 | bytes 180284 | tf_op jit(solution)/shard_map/mul | solution.py:162
  488.2 36.0 %while.62 = (s32[]{:T(128)}, f32[4,8,3,256]{3,1,0,2:T(8,128)}, s32[4,8,128]{2,1,0:T(8,128)S(1)}, f32[9,4096]{1,0:T(8,128)S(1)}, s32[4,8]{1,0:T(4,128)S(1)}, /*index=5*/s32[]{:T(128)}) while((s32[]{:T(128)}, f32[4,8,3,256]{3,1,0,2:T(8,128)}, s32[4,8,128]{2,1,0:T(8,128)S(1)}, f32[9,4096]{1,0:T(8,128)S(1)}, s32[4,8]{1,0:T(4,128)S(1)}, ...), condition=%wide.region_18.19_spmd.clone, body=%wide.region_17.18_spmd.clone.sunk | while | flops 876660928 | bytes 2507605 | solution.py:301
  (316 shorter events, 214.1 us)
Async XLA Ops:
  63.2 8.9 %copy-start.5 = (f32[2,6]{1,0:T(2,128)S(1)}, f32[2,6]{1,0:T(2,128)}, u32[]{:S(2)}) copy-start(f32[2,6]{1,0:T(2,128)} %param.25) | copy-start | bytes 148
  63.2 14.1 %copy-start.10 = (f32[1,3]{1,0:T(1,128)S(1)}, f32[1,3]{1,0:T(1,128)}, u32[]{:S(2)}) copy-start(f32[1,3]{1,0:T(1,128)} %constant.324.clone.1) | copy-start | bytes 40
  63.2 14.1 %copy-start.11 = (f32[1,3]{1,0:T(1,128)S(1)}, f32[1,3]{1,0:T(1,128)}, u32[]{:S(2)}) copy-start(f32[1,3]{1,0:T(1,128)} %constant.325.clone.1) | copy-start | bytes 40
  63.2 14.2 %copy-start.6 = (f32[1,3]{1,0:T(1,128)S(1)}, f32[1,3]{1,0:T(1,128)}, u32[]{:S(2)}) copy-start(f32[1,3]{1,0:T(1,128)} %constant.323.clone.1) | copy-start | bytes 40
  63.2 34.1 %copy-start.3 = (f32[32,3,256]{2,0,1:T(8,128)S(1)}, f32[32,3,256]{2,0,1:T(8,128)}, u32[]{:S(2)}) copy-start(f32[32,3,256]{2,0,1:T(8,128)} %param.32) | copy-start | bytes 294916
  63.2 34.1 %copy-start.8 = (s32[32]{0:T(128)S(1)}, s32[32]{0:T(128)}, u32[]{:S(2)}) copy-start(s32[32]{0:T(128)} %param.30) | copy-start | bytes 388
  64.8 33.5 %all-to-all-start = ((f32[59,32,128]{2,0,1:T(8,128)}), f32[59,32,128]{2,0,1:T(8,128)S(1)}, u32[]{:S(2)}, u32[]{:S(2)}) async-start(f32[59,32,128]{2,0,1:T(8,128)} %copy.48), calls=%async_computation | async-start | bytes 2097152 | tf_op jit(solution)/shard_map/all_to_all | solution.py:385
  92.2 18.3 %copy-start.1 = (s32[32,128]{1,0:T(8,128)S(1)}, s32[32,128]{1,0:T(8,128)}, u32[]{:S(2)}) copy-start(s32[32,128]{1,0:T(8,128)} %param.28) | copy-start | bytes 49156
  238.0 24.8 %copy-start.4 = (s32[1,4096]{1,0:T(1,128)S(1)}, s32[1,4096]{1,0:T(1,128)}, u32[]{:S(2)}) copy-start(s32[1,4096]{1,0:T(1,128)} %param.26) | copy-start | bytes 49156
  257.8 31.2 %all-to-all-start.1 = ((f32[32,59,128]{2,1,0:T(8,128)}), f32[32,59,128]{2,1,0:T(8,128)S(1)}, u32[]{:S(2)}, u32[]{:S(2)}) async-start(f32[32,59,128]{2,1,0:T(8,128)} %constant_dynamic-update-slice_fusion), calls=%async_computation.1 | async-start | bytes 2097152 | tf_op jit(solution)/shard_map/all_to_all | solution.py:38
  289.8 86.2 %copy-start = (f32[59,8192]{1,0:T(8,128)S(1)}, f32[59,8192]{1,0:T(8,128)}, u32[]{:S(2)}) copy-start(f32[59,8192]{1,0:T(8,128)} %get-tuple-element.1086) | copy-start | bytes 5799940
  289.8 86.2 %copy-start.7 = (f32[59]{0:T(128)S(1)}, f32[59]{0:T(128)}, u32[]{:S(2)}) copy-start(f32[59]{0:T(128)} %constant.528) | copy-start | bytes 712
  444.0 29.9 %copy-start.9 = (s32[32]{0:T(128)S(1)}, s32[32]{0:T(128)}, u32[]{:S(2)}) copy-start(s32[32]{0:T(128)} %param.31) | copy-start | bytes 388
  445.6 30.0 %all-to-all-start.2 = ((f32[59,32,128]{2,0,1:T(8,128)}), f32[59,32,128]{2,0,1:T(8,128)S(1)}, u32[]{:S(2)}, u32[]{:S(2)}) async-start(f32[59,32,128]{2,0,1:T(8,128)} %copy.57), calls=%async_computation.2 | async-start | bytes 2097152 | tf_op jit(solution)/shard_map/all_to_all | solution.py:398
  449.4 38.7 %copy-start.2 = (s32[32,128]{1,0:T(8,128)S(1)}, s32[32,128]{1,0:T(8,128)}, u32[]{:S(2)}) copy-start(s32[32,128]{1,0:T(8,128)} %param.29) | copy-start | bytes 49156
